TPU v7x, 32 devices: a whole 2x2x4 slice. The times are simulated.
32 devices in a mesh: lat: 4 (over y, x), lon: 8 (over z, core).
Axes of the slice: x: 2, y: 2, z: 4, core: 2. Of those that a mesh axis runs over, the one named last changes fastest.
Arguments:
- adjoint_in: bfloat16 [8, 100, 8, 1024], P(None, None, 'lat', 'lon'), may hold values from -6 to 6
- state: bfloat16 [2, 8, 100, 8, 1024], P(None, None, None, 'lat', 'lon'), may hold values from 0.29882812 to 1
- inverses: bfloat16 [3, 8, 100, 100], replicated
- courant_lon: float32 [8, 1024], P('lat', 'lon'), may hold values from 0.1 to 0.4
- courant_lat: float32 [8, 1024], P('lat', 'lon'), may hold values from 0.1 to 0.4
- emission: float32 [100, 8, 1024], P(None, 'lat', 'lon'), may hold values from 0.02 to 0.2
- region_id: int32 [8, 1024], P('lat', 'lon'), may hold values from 0 to 31, as said below
- stiffness: int32 [8, 8, 1024], P(None, 'lat', 'lon'), may hold values from 1 to 3
Outputs:
- adjoint_out: bfloat16 [8, 100, 8, 1024], P(None, None, 'lat', 'lon')
- emission_grad: float32 [32, 100], P(('lat', 'lon'))
Inputs may be any that keep to these rules, and one draw needn't show every extreme that they name: `region_id`: constant on aligned tiles of 2 x 2 columns.
All inputs are finite; a program needn't handle non-finite values.
Results may differ from a plain program's by a relative error of at most 0.0048.
Values sent between devices are 32-bit elements; how exact they have to be, the bound alone decides.
A program may use at most 64 MiB of HBM per device.

v0:
```python
import jax
import jax.numpy as jnp
from jax import lax
from jax.sharding import PartitionSpec as P

STEPS = 3
NWIN = 2
ADV = 2
REG_DEV = 1


def shifted(block, axis, distance):
    devices = range(lax.axis_size(axis))
    route = [((i - distance) % len(devices), i) for i in devices]
    return lax.ppermute(block, axis, route)


def from_behind(block, axis, distance):
    devices = range(lax.axis_size(axis))
    route = [(i - distance, i) for i in devices if i - distance in devices]
    return lax.ppermute(block, axis, route)


def advect(lam, clon, clat, east, south):
    right = jnp.concatenate([lam[:, :, :, 1:], east], axis=3)
    down = jnp.concatenate([lam[:, :, 1:, :], south], axis=2)
    return (1.0 - clon - clat) * lam + clat * down + clon * right


def transport_each(lam, courant_lon, courant_lat):
    for k in range(ADV):
        east = shifted(lam[:, :, :, :1], "lon", -1)
        south = from_behind(lam[:, :, :1, :], "lat", -1)
        lam = advect(lam, courant_lon, courant_lat, east, south)
    return lam


def transposed(mats, right_side):
    return lax.dot_general(
        mats, right_side, (((1,), (1,)), ((0,), (0,))), preferred_element_type=jnp.float32
    )


def chemistry(lam, factor, inverses, stiffness):
    levels, spec, rows, cols = lam.shape
    flat = lam.reshape(levels, spec, rows * cols)
    yfac = factor.reshape(levels, spec, rows * cols)
    live = stiffness.reshape(levels, 1, rows * cols)
    for s in reversed(range(STEPS)):
        mats = inverses[s]

        def advance(values, mats=mats, s=s):
            first = transposed(mats, values.astype(jnp.bfloat16))
            second = transposed(mats, (first * yfac).astype(jnp.bfloat16))
            third = transposed(mats, (second * yfac).astype(jnp.bfloat16))
            cand = 0.4 * values + 0.3 * first + 0.2 * second + 0.1 * third
            return jnp.where(live > s, cand, values)

        flat = lax.cond(jnp.any(stiffness > s), advance, lambda values: values, flat)
    return flat.reshape(levels, spec, rows, cols)


def per_device(
    adjoint_in, state, inverses, courant_lon, courant_lat, emission, region_id, stiffness
):
    lam = adjoint_in.astype(jnp.float32)
    surface = jnp.zeros(emission.shape, jnp.float32)
    for window in reversed(range(NWIN)):
        lam = transport_each(lam, courant_lon, courant_lat)
        lam = chemistry(lam, state[window], inverses, stiffness)
        surface = surface + lam[0]
    spec = emission.shape[0]
    regions = REG_DEV * lax.axis_size("lat") * lax.axis_size("lon")
    contrib = (surface * emission).reshape(spec, -1)
    labels = lax.broadcasted_iota(jnp.int32, (regions, contrib.shape[1]), 0)
    onehot = (region_id.reshape(1, -1) == labels).astype(jnp.float32)
    partial_value = lax.dot_general(
        onehot,
        contrib,
        (((1,), (1,)), ((), ())),
        precision=lax.Precision.HIGHEST,
        preferred_element_type=jnp.float32,
    )
    total = lax.psum(partial_value, ("lat", "lon"))
    share = REG_DEV
    grad = lax.dynamic_slice_in_dim(total, lax.axis_index(("lat", "lon")) * share, share, 0)
    return (lam.astype(jnp.bfloat16), grad)


def solution(mesh):
    in_specs = (
        P(None, None, "lat", "lon"),
        P(None, None, None, "lat", "lon"),
        P(),
        P("lat", "lon"),
        P("lat", "lon"),
        P(None, "lat", "lon"),
        P("lat", "lon"),
        P(None, "lat", "lon"),
    )
    out_specs = (P(None, None, "lat", "lon"), P(("lat", "lon"), None))
    return jax.shard_map(
        per_device, mesh=mesh, in_specs=in_specs, out_specs=out_specs, check_vma=False
    )
```

profile of v0, /device:TPU:0, one launch (start us, length us, event | category | flops | bytes accessed | tf_op | source)
XLA Modules:
  0.0 119.0 jit_solution(164117389838447661)
XLA Ops:
  0.6 1.1 copy_convert_fusion.5
  1.7 0.8 fusion.83
  2.5 1.3 %collective-permute-start = (f32[8,100,1,128]{3,0,2,1:T(8,128)}, f32[8,100,1,128]{3,0,2,1:T(8,128)}, u32[]{:S(2)}, u32[]{:S(2)}) collective-permute-start(f32[8,100,1,128]{3,0,2,1:T(8,128)} %get-tuple-element.166), channel_id=1, source_target_pairs={{8,0},{16,8},{24,16},{9,1},{17,9},{25,17},{10,2},{18,10},{26,18},{... | collective-permute-start | bytes 1228808 | tf_op jit(solution)/shard_map/ppermute | solution.py:21
  3.8 0.4 copy.34
  4.2 4.5 %collective-permute-start.1 = (f32[8,100,2,1]{1,0,3,2:T(8,128)S(1)}, f32[8,100,2,1]{1,0,3,2:T(8,128)S(1)}, u32[]{:S(2)}, u32[]{:S(2)}) collective-permute-start(f32[8,100,2,1]{1,0,3,2:T(8,128)S(1)} %copy.34), channel_id=1, source_target_pairs={{1,0},{2,1},{3,2},{4,3},{5,4},{6,5},{7,6},{0,7},{9,8},{10,9},{11,1... | collective-permute-start | bytes 19208 | tf_op jit(solution)/shard_map/ppermute | solution.py:15
  8.7 0.3 slice.99
  9.0 1.1 collective-permute-done.1
  10.1 0.5 copy.35
  10.5 6.6 %collective-permute-done = f32[8,100,1,128]{3,0,2,1:T(8,128)} collective-permute-done((f32[8,100,1,128]{3,0,2,1:T(8,128)}, f32[8,100,1,128]{3,0,2,1:T(8,128)}, u32[]{:S(2)}, u32[]{:S(2)}) %collective-permute-start) | collective-permute-done | bytes 409632 | tf_op jit(solution)/shard_map/ppermute | solution.py:21
  17.1 1.3 %fusion.65 = f32[8,100,2,128]{3,0,2,1:T(8,128)S(1)} fusion(f32[8,100,1,128]{3,0,2,1:T(8,128)} %collective-permute-done, f32[8,100,1,128]{3,0,2,1:T(8,128)S(1)} %get-tuple-element.165, f32[8,100,2,1]{3,0,2,1:T(8,128)S(1)} %copy.35, f32[8,100,2,127]{3,0,2,1:T(8,128)S(1)} %slice.99, f32[2,128]{1,0:T(2,128)S(1)} %copy-done.7, f32[2,128]{1,0:T(2,128)S(1)} %copy-done.8, ...), kind=kLoop, calls=%fused_computation.86 | loop fusion | flops 1638400 | bytes 2870272 | tf_op jit(solution)/shard_map/add | solution.py:27
  18.5 0.9 fusion.82
  19.4 1.4 %collective-permute-start.2 = (f32[8,100,1,128]{3,0,2,1:T(8,128)}, f32[8,100,1,128]{3,0,2,1:T(8,128)}, u32[]{:S(2)}, u32[]{:S(2)}) collective-permute-start(f32[8,100,1,128]{3,0,2,1:T(8,128)} %get-tuple-element.164), channel_id=1, source_target_pairs={{8,0},{16,8},{24,16},{9,1},{17,9},{25,17},{10,2},{18,10},{26,18},{... | collective-permute-start | bytes 1228808 | tf_op jit(solution)/shard_map/ppermute | solution.py:21
  20.9 1.3 %fusion.79 = (bf16[1,8,100,2,128]{4,3,2,1,0:T(2,128)(2,1)}, bf16[1,8,100,2,128]{4,3,2,1,0:T(2,128)(2,1)S(1)}) fusion(bf16[2,8,100,2,128]{4,3,2,1,0:T(2,128)(2,1)S(1)} %copy-done.3), kind=kLoop, calls=%fused_computation.122 | loop fusion | bytes 1638400 | tf_op jit(solution)/shard_map/slice | solution.py:70
  22.3 0.4 copy.36
  22.6 2.4 %collective-permute-start.3 = (f32[8,100,2,1]{1,0,3,2:T(8,128)S(1)}, f32[8,100,2,1]{1,0,3,2:T(8,128)}, u32[]{:S(2)}, u32[]{:S(2)}) collective-permute-start(f32[8,100,2,1]{1,0,3,2:T(8,128)S(1)} %copy.36), channel_id=1, source_target_pairs={{1,0},{2,1},{3,2},{4,3},{5,4},{6,5},{7,6},{0,7},{9,8},{10,9},{11,1... | collective-permute-start | bytes 19208 | tf_op jit(solution)/shard_map/ppermute | solution.py:15
  25.1 0.7 compare_reduce_fusion
  28.5 0.3 slice.103
  28.8 1.1 copy.37
  30.0 3.0 %collective-permute-done.2 = f32[8,100,1,128]{3,0,2,1:T(8,128)} collective-permute-done((f32[8,100,1,128]{3,0,2,1:T(8,128)}, f32[8,100,1,128]{3,0,2,1:T(8,128)}, u32[]{:S(2)}, u32[]{:S(2)}) %collective-permute-start.2) | collective-permute-done | bytes 409632 | tf_op jit(solution)/shard_map/ppermute | solution.py:21
  33.0 1.4 %fusion.68 = f32[8,100,256]{2,0,1:T(8,128)S(1)} fusion(f32[8,100,1,128]{3,0,2,1:T(8,128)} %collective-permute-done.2, f32[8,100,1,128]{3,0,2,1:T(8,128)} %get-tuple-element.163, f32[8,100,2,1]{3,0,2,1:T(8,128)S(1)} %copy.37, f32[8,100,2,127]{3,0,2,1:T(8,128)S(1)} %slice.103, f32[8,100,2,128]{3,0,2,1:T(8,128)S(1)} %fusion.65, f32[2,128]{1,0:T(2,128)S(1)} %copy-done.7, ...), kind=kLoop, calls=%fused_computation.91 | loop fusion | flops 1433600 | bytes 3279872 | tf_op jit(solution)/shard_map/reshape | solution.py:46
  34.4 1.3 %conditional.6 = (f32[8,100,256]{2,1,0:T(8,128)S(1)}) conditional(s32[]{:T(128)} %convert_element_type.102, (f32[8,100,256]{2,0,1:T(8,128)S(1)}) %tuple.65, (s32[8,1,256]{2,0,1:T(8,128)S(1)}, f32[8,100,256]{2,0,1:T(8,128)S(1)}, bf16[8,100,100]{1,2,0:T(8,128)(2,1)S(1)}, bf16[8,100,256]{2,0,1:T(8,128)(2,1)S(1)}) %tuple.94), branch_computations={%region_3.4_spmd, %region_4.5_spmd} | conditional | flops 125749248 | bytes 7865096 | solution.py:59
  34.5 0.4 fusion.5
  34.9 0.3 convolution_bitcast_fusion
  35.2 0.6 fusion.2
  35.8 1.3 %conditional.7 = (f32[8,100,256]{2,1,0:T(8,128)S(1)}) conditional(s32[]{:T(128)} %convert_element_type.101, f32[8,100,256]{2,1,0:T(8,128)S(1)} %get-tuple-element.170, (s32[8,1,256]{2,0,1:T(8,128)S(1)}, f32[8,100,256]{2,1,0:T(8,128)S(1)}, bf16[8,100,100]{1,2,0:T(8,128)(2,1)S(1)}, bf16[8,100,256]{2,0,1:T(8,128)(2,1)S(1)}) %tuple.98), branch_computations={%region_5.6_spmd, %region_6.7_spmd} | conditional | flops 125954048 | bytes 7865096 | solution.py:59
  36.1 0.3 convolution_bitcast_fusion.1
  36.4 0.8 fusion.12
  37.1 1.3 %conditional.8 = (f32[8,100,256]{2,1,0:T(8,128)S(1)}) conditional(s32[]{:T(128)} %convert_element_type.100, f32[8,100,256]{2,1,0:T(8,128)S(1)} %get-tuple-element.171, (s32[8,1,256]{2,0,1:T(8,128)S(1)}, f32[8,100,256]{2,1,0:T(8,128)S(1)}, bf16[8,100,100]{1,2,0:T(8,128)(2,1)S(1)}, bf16[8,100,256]{2,0,1:T(8,128)(2,1)S(1)}) %tuple.96), branch_computations={%region_7.8_spmd, %region_8.9_spmd} | conditional | flops 125954048 | bytes 7865096 | solution.py:59
  37.4 0.3 convolution_bitcast_fusion.2
  37.7 0.8 fusion.23
  38.7 0.8 fusion.81
  39.5 1.3 %collective-permute-start.4 = (f32[8,100,1,128]{3,0,2,1:T(8,128)}, f32[8,100,1,128]{3,0,2,1:T(8,128)}, u32[]{:S(2)}, u32[]{:S(2)}) collective-permute-start(f32[8,100,1,128]{3,0,2,1:T(8,128)} %get-tuple-element.162), channel_id=1, source_target_pairs={{8,0},{16,8},{24,16},{9,1},{17,9},{25,17},{10,2},{18,10},{26,18},{... | collective-permute-start | bytes 1228808 | tf_op jit(solution)/shard_map/ppermute | solution.py:21
  40.8 1.0 copy.49
  41.8 0.3 slice.107
  42.1 1.3 %collective-permute-done.5 = f32[8,100,2,1]{1,0,3,2:T(8,128)} collective-permute-done((f32[8,100,2,1]{1,0,3,2:T(8,128)}, f32[8,100,2,1]{1,0,3,2:T(8,128)}, u32[]{:S(2)}, u32[]{:S(2)}) %collective-permute-start.5) | collective-permute-done | bytes 6432 | tf_op jit(solution)/shard_map/ppermute | solution.py:15
  43.4 2.0 %copy.50 = f32[8,100,2,1]{3,0,2,1:T(8,128)} copy(f32[8,100,2,1]{1,0,3,2:T(8,128)} %collective-permute-done.5) | data formatting | bytes 12800 | tf_op jit(solution)/shard_map/ppermute | solution.py:15
  45.4 6.8 %collective-permute-done.4 = f32[8,100,1,128]{3,0,2,1:T(8,128)} collective-permute-done((f32[8,100,1,128]{3,0,2,1:T(8,128)}, f32[8,100,1,128]{3,0,2,1:T(8,128)}, u32[]{:S(2)}, u32[]{:S(2)}) %collective-permute-start.4) | collective-permute-done | bytes 409632 | tf_op jit(solution)/shard_map/ppermute | solution.py:21
  52.1 1.7 %multiply_add_fusion = f32[8,100,2,128]{3,0,2,1:T(8,128)S(1)} fusion(f32[8,100,1,128]{3,0,2,1:T(8,128)} %collective-permute-done.4, f32[8,100,1,128]{3,0,2,1:T(8,128)S(1)} %get-tuple-element.161, f32[2,128]{1,0:T(2,128)S(1)} %copy-done.7, f32[2,128]{1,0:T(2,128)S(1)} %copy-done.8, f32[2,128]{1,0:T(2,128)S(1)} %copy-done.11, f32[8,100,2,1]{3,0,2,1:T(8,128)} %copy.50, ...), kind=kLoop, calls=%fused_computation.107 | loop fusion | flops 1433600 | bytes 3279872 | tf_op jit(solution)/shard_map/add | solution.py:27
  53.8 0.9 fusion.80
  54.8 1.3 %collective-permute-start.6 = (f32[8,100,1,128]{3,0,2,1:T(8,128)}, f32[8,100,1,128]{3,0,2,1:T(8,128)}, u32[]{:S(2)}, u32[]{:S(2)}) collective-permute-start(f32[8,100,1,128]{3,0,2,1:T(8,128)} %get-tuple-element.160), channel_id=1, source_target_pairs={{8,0},{16,8},{24,16},{9,1},{17,9},{25,17},{10,2},{18,10},{26,18},{... | collective-permute-start | bytes 1228808 | tf_op jit(solution)/shard_map/ppermute | solution.py:21
  56.1 1.0 copy.51
  57.0 1.4 %collective-permute-start.7 = (f32[8,100,2,1]{1,0,3,2:T(8,128)}, f32[8,100,2,1]{1,0,3,2:T(8,128)}, u32[]{:S(2)}, u32[]{:S(2)}) collective-permute-start(f32[8,100,2,1]{1,0,3,2:T(8,128)} %copy.51), channel_id=1, source_target_pairs={{1,0},{2,1},{3,2},{4,3},{5,4},{6,5},{7,6},{0,7},{9,8},{10,9},{11,1... | collective-permute-start | bytes 19208 | tf_op jit(solution)/shard_map/ppermute | solution.py:15
  58.4 1.1 copy.137
  59.5 1.2 %slice.111 = f32[8,100,2,127]{3,0,2,1:T(8,128)} slice(f32[8,100,2,128]{3,0,2,1:T(8,128)S(1)} %multiply_add_fusion), slice={[0:8], [0:100], [0:2], [1:128]} | slice | bytes 1625600 | tf_op jit(solution)/shard_map/slice | solution.py:25
  60.7 2.0 %copy.52 = f32[8,100,2,1]{3,0,2,1:T(8,128)} copy(f32[8,100,2,1]{1,0,3,2:T(8,128)} %collective-permute-done.7) | data formatting | bytes 12800 | tf_op jit(solution)/shard_map/ppermute | solution.py:15
  62.7 3.8 %collective-permute-done.6 = f32[8,100,1,128]{3,0,2,1:T(8,128)} collective-permute-done((f32[8,100,1,128]{3,0,2,1:T(8,128)}, f32[8,100,1,128]{3,0,2,1:T(8,128)}, u32[]{:S(2)}, u32[]{:S(2)}) %collective-permute-start.6) | collective-permute-done | bytes 409632 | tf_op jit(solution)/shard_map/ppermute | solution.py:21
  66.5 0.7 copy-done.12
  67.2 2.5 %fusion.71 = f32[8,100,256]{2,0,1:T(8,128)S(1)} fusion(f32[8,100,1,128]{3,0,2,1:T(8,128)} %collective-permute-done.6, f32[8,100,1,128]{3,0,2,1:T(8,128)} %get-tuple-element.159, f32[8,100,2,1]{3,0,2,1:T(8,128)} %copy.52, f32[8,100,2,127]{3,0,2,1:T(8,128)} %slice.111, f32[8,100,256]{2,1,0:T(8,128)S(1)} %get-tuple-element.172, ...), kind=kLoop, calls=%fused_computation.98 | loop fusion | flops 2867200 | bytes 4918272 | tf_op jit(solution)/shard_map/add | solution.py:27
  69.7 1.5 %conditional.9 = (f32[8,100,256]{2,1,0:T(8,128)S(1)}) conditional(s32[]{:T(128)} %convert_element_type.102, (f32[8,100,256]{2,0,1:T(8,128)S(1)}) %tuple.66, (s32[8,1,256]{2,0,1:T(8,128)S(1)}, f32[8,100,256]{2,0,1:T(8,128)S(1)}, bf16[8,100,100]{1,2,0:T(8,128)(2,1)S(1)}, bf16[8,100,256]{2,0,1:T(8,128)(2,1)S(1)}) %tuple.95), branch_computations={%region_9.10_spmd, %region_10.11_spmd} | conditional | flops 125749248 | bytes 7865096 | solution.py:59
  69.9 0.4 fusion.37
  70.3 0.3 convolution_bitcast_fusion.3
  70.6 0.6 fusion.34
  71.2 1.3 %conditional.10 = (f32[8,100,256]{2,1,0:T(8,128)S(1)}) conditional(s32[]{:T(128)} %convert_element_type.101, f32[8,100,256]{2,1,0:T(8,128)S(1)} %get-tuple-element.173, (s32[8,1,256]{2,0,1:T(8,128)S(1)}, f32[8,100,256]{2,1,0:T(8,128)S(1)}, bf16[8,100,100]{1,2,0:T(8,128)(2,1)S(1)}, bf16[8,100,256]{2,0,1:T(8,128)(2,1)S(1)}) %tuple.99), branch_computations={%region_11.12_spmd, %region_12.13_spmd} | conditional | flops 125954048 | bytes 7865096 | solution.py:59
  71.2 0.3 fusion.49
  71.5 0.3 convolution_bitcast_fusion.4
  71.8 0.8 fusion.44
  72.5 1.3 %conditional.11 = (f32[8,100,256]{2,1,0:T(8,128)S(1)}) conditional(s32[]{:T(128)} %convert_element_type.100, f32[8,100,256]{2,1,0:T(8,128)S(1)} %get-tuple-element.174, (s32[8,1,256]{2,0,1:T(8,128)S(1)}, f32[8,100,256]{2,1,0:T(8,128)S(1)}, bf16[8,100,100]{1,2,0:T(8,128)(2,1)S(1)}, bf16[8,100,256]{2,0,1:T(8,128)(2,1)S(1)}) %tuple.97), branch_computations={%region_13.14_spmd, %region_14.15_spmd} | conditional | flops 125954048 | bytes 7865096 | solution.py:59
  72.8 0.3 convolution_bitcast_fusion.5
  73.1 0.8 fusion.55
  74.2 0.8 copy-done.5
  75.2 0.7 copy-done.13
  76.0 41.4 %psum.7 = f32[32,100]{1,0:T(8,128)S(1)} all-reduce(f32[32,100]{1,0:T(8,128)S(1)} %fusion.77), channel_id=1, replica_groups=mesh['lat'=4,'lon'=8] {'lat','lon'}, use_global_device_ids=true, to_apply=%region_15.16 | all-reduce | flops 3200 | bytes 25600 | tf_op jit(solution)/shard_map/psum | solution.py:84
  117.4 1.1 copy.60
  118.5 0.5 constant_dynamic-slice_fusion
  (52 shorter events, 2.6 us)
Async XLA Ops:
  2.5 14.6 %collective-permute-start = (f32[8,100,1,128]{3,0,2,1:T(8,128)}, f32[8,100,1,128]{3,0,2,1:T(8,128)}, u32[]{:S(2)}, u32[]{:S(2)}) collective-permute-start(f32[8,100,1,128]{3,0,2,1:T(8,128)} %get-tuple-element.166), channel_id=1, source_target_pairs={{8,0},{16,8},{24,16},{9,1},{17,9},{25,17},{10,2},{18,10},{26,18},{... | collective-permute-start | bytes 1228808 | tf_op jit(solution)/shard_map/ppermute | solution.py:21
  3.8 4.9 %copy-start.7 = (f32[2,128]{1,0:T(2,128)S(1)}, f32[2,128]{1,0:T(2,128)}, u32[]{:S(2)}) copy-start(f32[2,128]{1,0:T(2,128)} %param.23) | copy-start | bytes 3076
  3.8 4.9 %copy-start.8 = (f32[2,128]{1,0:T(2,128)S(1)}, f32[2,128]{1,0:T(2,128)}, u32[]{:S(2)}) copy-start(f32[2,128]{1,0:T(2,128)} %param.24) | copy-start | bytes 3076
  4.2 5.9 %collective-permute-start.1 = (f32[8,100,2,1]{1,0,3,2:T(8,128)S(1)}, f32[8,100,2,1]{1,0,3,2:T(8,128)S(1)}, u32[]{:S(2)}, u32[]{:S(2)}) collective-permute-start(f32[8,100,2,1]{1,0,3,2:T(8,128)S(1)} %copy.34), channel_id=1, source_target_pairs={{1,0},{2,1},{3,2},{4,3},{5,4},{6,5},{7,6},{0,7},{9,8},{10,9},{11,1... | collective-permute-start | bytes 19208 | tf_op jit(solution)/shard_map/ppermute | solution.py:15
  8.7 8.4 %copy-start.9 = (f32[2,128]{1,0:T(2,128)}, f32[2,128]{1,0:T(2,128)S(1)}, u32[]{:S(2)}) copy-start(f32[2,128]{1,0:T(2,128)S(1)} %subtract_subtract_fusion) | copy-start | bytes 3076
  9.0 8.1 %copy-start.2 = (bf16[8,100,2,128]{3,2,1,0:T(2,128)(2,1)S(1)}, bf16[8,100,2,128]{3,2,1,0:T(2,128)(2,1)}, u32[]{:S(2)}) copy-start(bf16[8,100,2,128]{3,2,1,0:T(2,128)(2,1)} %param.20) | copy-start | bytes 1228804
  18.5 2.4 %copy-start.4 = (bf16[3,8,100,100]{3,1,2,0:T(8,128)(2,1)S(1)}, bf16[3,8,100,100]{3,1,2,0:T(8,128)(2,1)}, u32[]{:S(2)}) copy-start(bf16[3,8,100,100]{3,1,2,0:T(8,128)(2,1)} %param.22) | copy-start | bytes 1440004
  19.4 1.5 %copy-start.3 = (bf16[2,8,100,2,128]{4,3,2,1,0:T(2,128)(2,1)S(1)}, bf16[2,8,100,2,128]{4,3,2,1,0:T(2,128)(2,1)}, u32[]{:S(2)}) copy-start(bf16[2,8,100,2,128]{4,3,2,1,0:T(2,128)(2,1)} %param.21) | copy-start | bytes 2457604
  19.4 13.6 %collective-permute-start.2 = (f32[8,100,1,128]{3,0,2,1:T(8,128)}, f32[8,100,1,128]{3,0,2,1:T(8,128)}, u32[]{:S(2)}, u32[]{:S(2)}) collective-permute-start(f32[8,100,1,128]{3,0,2,1:T(8,128)} %get-tuple-element.164), channel_id=1, source_target_pairs={{8,0},{16,8},{24,16},{9,1},{17,9},{25,17},{10,2},{18,10},{26,18},{... | collective-permute-start | bytes 1228808 | tf_op jit(solution)/shard_map/ppermute | solution.py:21
  22.3 2.8 %copy-start.6 = (s32[8,2,128]{2,1,0:T(2,128)S(1)}, s32[8,2,128]{2,1,0:T(2,128)}, u32[]{:S(2)}) copy-start(s32[8,2,128]{2,1,0:T(2,128)} %param.27) | copy-start | bytes 24580
  22.6 6.2 %collective-permute-start.3 = (f32[8,100,2,1]{1,0,3,2:T(8,128)S(1)}, f32[8,100,2,1]{1,0,3,2:T(8,128)}, u32[]{:S(2)}, u32[]{:S(2)}) collective-permute-start(f32[8,100,2,1]{1,0,3,2:T(8,128)S(1)} %copy.36), channel_id=1, source_target_pairs={{1,0},{2,1},{3,2},{4,3},{5,4},{6,5},{7,6},{0,7},{9,8},{10,9},{11,1... | collective-permute-start | bytes 19208 | tf_op jit(solution)/shard_map/ppermute | solution.py:15
  30.0 3.0 %copy-start.10 = (f32[2,128]{1,0:T(2,128)S(1)}, f32[2,128]{1,0:T(2,128)}, u32[]{:S(2)}) copy-start(f32[2,128]{1,0:T(2,128)} %copy-done.9) | copy-start | bytes 3076
  39.5 12.6 %copy-start.1 = (f32[8,100,1,128]{3,0,2,1:T(8,128)}, f32[8,100,1,128]{3,0,2,1:T(8,128)S(1)}, u32[]{:S(2)}) copy-start(f32[8,100,1,128]{3,0,2,1:T(8,128)S(1)} %get-tuple-element.161) | copy-start | bytes 1228804
  39.5 12.6 %collective-permute-start.4 = (f32[8,100,1,128]{3,0,2,1:T(8,128)}, f32[8,100,1,128]{3,0,2,1:T(8,128)}, u32[]{:S(2)}, u32[]{:S(2)}) collective-permute-start(f32[8,100,1,128]{3,0,2,1:T(8,128)} %get-tuple-element.162), channel_id=1, source_target_pairs={{8,0},{16,8},{24,16},{9,1},{17,9},{25,17},{10,2},{18,10},{26,18},{... | collective-permute-start | bytes 1228808 | tf_op jit(solution)/shard_map/ppermute | solution.py:21
  41.8 1.6 %collective-permute-start.5 = (f32[8,100,2,1]{1,0,3,2:T(8,128)}, f32[8,100,2,1]{1,0,3,2:T(8,128)}, u32[]{:S(2)}, u32[]{:S(2)}) collective-permute-start(f32[8,100,2,1]{1,0,3,2:T(8,128)} %copy.49), channel_id=1, source_target_pairs={{1,0},{2,1},{3,2},{4,3},{5,4},{6,5},{7,6},{0,7},{9,8},{10,9},{11,1... | collective-permute-start | bytes 19208 | tf_op jit(solution)/shard_map/ppermute | solution.py:15
  45.4 6.8 %copy-start.11 = (f32[2,128]{1,0:T(2,128)S(1)}, f32[2,128]{1,0:T(2,128)}, u32[]{:S(2)}) copy-start(f32[2,128]{1,0:T(2,128)} %copy-done.9) | copy-start | bytes 3076
  54.8 11.7 %collective-permute-start.6 = (f32[8,100,1,128]{3,0,2,1:T(8,128)}, f32[8,100,1,128]{3,0,2,1:T(8,128)}, u32[]{:S(2)}, u32[]{:S(2)}) collective-permute-start(f32[8,100,1,128]{3,0,2,1:T(8,128)} %get-tuple-element.160), channel_id=1, source_target_pairs={{8,0},{16,8},{24,16},{9,1},{17,9},{25,17},{10,2},{18,10},{26,18},{... | collective-permute-start | bytes 1228808 | tf_op jit(solution)/shard_map/ppermute | solution.py:21
  57.0 3.7 %collective-permute-start.7 = (f32[8,100,2,1]{1,0,3,2:T(8,128)}, f32[8,100,2,1]{1,0,3,2:T(8,128)}, u32[]{:S(2)}, u32[]{:S(2)}) collective-permute-start(f32[8,100,2,1]{1,0,3,2:T(8,128)} %copy.51), channel_id=1, source_target_pairs={{1,0},{2,1},{3,2},{4,3},{5,4},{6,5},{7,6},{0,7},{9,8},{10,9},{11,1... | collective-permute-start | bytes 19208 | tf_op jit(solution)/shard_map/ppermute | solution.py:15
  60.7 5.8 %copy-start = (f32[8,100,2,1]{3,0,2,1:T(8,128)S(1)}, f32[8,100,2,1]{3,0,2,1:T(8,128)}, u32[]{:S(2)}) copy-start(f32[8,100,2,1]{3,0,2,1:T(8,128)} %copy.50) | copy-start | bytes 19204
  66.5 0.7 copy-start.12
  74.1 0.9 copy-start.5
  75.2 0.7 copy-start.13
where the time goes:
time: 119 us
  blocking collectives  41.4 us (35%)
  waiting for transfers between devices  22.5 us (19%)
  local copies, waits for them, and re-layouts  21.5 us (18%)
  starting transfers between devices  13.6 us (11%)
  other arithmetic  8.79 us (7%)
  matrix products  7.96 us (7%)
  between operations  2.85 us (2%)
    psum x1, blocking collectives, per_device(): total = lax.psum(partial_value, ('lat', 'lon'))  41.4 us
    ppermute x4, waiting for transfers between devices, from_behind(): return lax.ppermute(block, axis, route)  20.1 us
    ppermute x4, starting transfers between devices, shifted(): return lax.ppermute(block, axis, route)  8.34 us
    dot_general x18, matrix products, transposed(): lax.dot_general(mats, right_side, (((1,), (1,)), ((0,), (0,))), preferred...  7.79 us
    ppermute x4, local copies, waits for them, and re-layouts, shifted(): return lax.ppermute(block, axis, route)  5.64 us
    add x3, other arithmetic, advect(): return (1.0 - clon - clat) * lam + clat * down + clon * right  5.49 us
    ppermute x4, starting transfers between devices, from_behind(): return lax.ppermute(block, axis, route)  5.25 us
    unnamed x36, local copies, waits for them, and re-layouts  5.18 us
  transfers between devices with their start and end apart: 8, of which 6 were waited for; matrix products, arithmetic and copies ran while one was open for 12% of the time, Pallas kernels for 0%

commit v1 on v0

v1 whole, which is shorter than its diff:
```python
import functools

import jax
import jax.numpy as jnp
from jax import lax
from jax.experimental import pallas as pl
from jax.experimental.pallas import tpu as pltpu
from jax.sharding import PartitionSpec as P

MESH = pl.DeviceIdType.MESH
LP = 2


def kernel(
    n_lat, n_lon,
    adj_hbm, state_hbm, inv_hbm, clon_ref, clat_ref, em_ref, reg_ref, stiff_ref,
    out_hbm, grad_ref,
    adj, state, inv, mats, lam_a, lam_b, west1, west2, south1, south2, east1, east2,
    tmp, fin, outbuf, coef, part, inbox1, turn, inbox2,
    adj_sem, state_sem, inv_sem, out_sem, send_sem, recv_sem, s1, r1, s2, r2,
):
    lev, rows2, cols = adj.shape
    nwin = state.shape[0]
    steps = inv.shape[0]
    spec = rows2 // 2
    per = lev // LP
    units = nwin * per
    lat, lon = lax.axis_index("lat"), lax.axis_index("lon")
    north = jnp.maximum(lat - 1, 0)
    west = lax.rem(lon + n_lon - 1, n_lon)
    has_north = lat > 0
    has_south = lat < n_lat - 1

    loads = [pltpu.make_async_copy(adj_hbm, adj, adj_sem)]
    loads[0].start()
    inv_load = pltpu.make_async_copy(inv_hbm, inv, inv_sem)
    inv_load.start()
    state_loads = [
        pltpu.make_async_copy(state_hbm.at[w], state.at[w], state_sem.at[w]) for w in range(nwin)
    ]
    for w in reversed(range(nwin)):
        state_loads[w].start()

    barrier = pltpu.get_barrier_semaphore()
    for k in range(1, n_lon):
        pl.semaphore_signal(barrier, inc=1, device_id=(lat, lax.rem(lon + k, n_lon)), device_id_type=MESH)
    for k in range(1, n_lat):
        pl.semaphore_signal(barrier, inc=1, device_id=(lax.rem(lat + k, n_lat), lon), device_id_type=MESH)

    for r in range(2):
        clon, clat = clon_ref[r:r + 1, :], clat_ref[r:r + 1, :]
        coef[0, r] = jnp.broadcast_to(1.0 - clon - clat, (8, cols))
        coef[1, r] = jnp.broadcast_to(clat, (8, cols))
        coef[2, r] = jnp.broadcast_to(clon, (8, cols))

    lane = lax.broadcasted_iota(jnp.int32, (spec, cols), 1)

    def weights(r):
        return coef[0, r, 0:1, :], coef[1, r, 0:1, :], coef[2, r, 0:1, :]

    def remote(kind, src, dst, u, device):
        return pltpu.make_async_remote_copy(
            src_ref=src.at[u], dst_ref=dst.at[u],
            send_sem=send_sem.at[kind, u], recv_sem=recv_sem.at[kind, u],
            device_id=device, device_id_type=MESH,
        )

    def row_copy(kind, u):
        src, dst = ((lam_a, south1), (lam_b, south2))[kind]
        return remote(kind, src.at[0], dst, u, (north, lon))

    def col_copy(kind, u):
        src, dst = ((west1, east1), (west2, east2))[kind]
        return remote(kind + 2, src, dst, u, (lat, west))

    def pack(row0, row1):
        return jnp.where(lane == 0, row0, pltpu.roll(row1, 1, 1))

    def shift(row0, row1, edge):
        right0 = pltpu.roll(jnp.where(lane == 0, edge, row0), cols - 1, 1)
        right1 = pltpu.roll(jnp.where(lane == 0, pltpu.roll(edge, cols - 1, 1), row1), cols - 1, 1)
        return right0, right1

    def launch(u):
        @pl.when(has_north)
        def _():
            row_copy(0, u).start()
        for p in range(LP):
            west1[u, p] = pack(lam_a[0, u, p], lam_a[1, u, p])
        col_copy(0, u).start()

    def first_step(u):
        col_copy(0, u).wait_recv()
        c0, a0, o0 = weights(0)
        c1, a1, o1 = weights(1)
        for p in range(LP):
            row0, row1 = lam_a[0, u, p], lam_a[1, u, p]
            right0, right1 = shift(row0, row1, east1[u, p])
            lam_b[0, u, p] = c0 * row0 + a0 * row1 + o0 * right0
            lam_b[1, u, p] = c1 * row1 + o1 * right1

        @pl.when(has_north)
        def _():
            row_copy(1, u).start()

        @pl.when(has_south)
        def _():
            row_copy(0, u).wait_recv()
        for p in range(LP):
            row1 = lam_b[1, u, p] + a1 * south1[u, p]
            lam_b[1, u, p] = row1
            west2[u, p] = pack(lam_b[0, u, p], row1)
        col_copy(1, u).start()

    def second_step(u):
        col_copy(1, u).wait_recv()

        @pl.when(has_south)
        def _():
            row_copy(1, u).wait_recv()
        c0, a0, o0 = weights(0)
        c1, a1, o1 = weights(1)
        window = nwin - 1 - u // per
        group = u % per
        flats, ys, lives = [], [], []
        for p in range(LP):
            level = group * LP + p
            row0, row1 = lam_b[0, u, p], lam_b[1, u, p]
            right0, right1 = shift(row0, row1, east2[u, p])
            new0 = c0 * row0 + a0 * row1 + o0 * right0
            new1 = c1 * row1 + a1 * south2[u, p] + o1 * right1
            flats.append(jnp.concatenate([new0, new1], axis=1))
            tmp[p] = state[window, level].astype(jnp.float32)
            ys.append(jnp.concatenate(
                [tmp[p, pl.ds(0, spec, stride=2), :], tmp[p, pl.ds(1, spec, stride=2), :]], axis=1))
            live = stiff_ref[level]
            lives.append(jnp.concatenate([live[0:1], live[1:2]], axis=1))
        for s in reversed(range(steps)):
            mat = [mats[s, group * LP + p] for p in range(LP)]
            v1 = [jnp.dot(mat[p], flats[p].astype(jnp.bfloat16), preferred_element_type=jnp.float32) for p in range(LP)]
            v2 = [jnp.dot(mat[p], (v1[p] * ys[p]).astype(jnp.bfloat16), preferred_element_type=jnp.float32) for p in range(LP)]
            v3 = [jnp.dot(mat[p], (v2[p] * ys[p]).astype(jnp.bfloat16), preferred_element_type=jnp.float32) for p in range(LP)]
            flats = [
                jnp.where(lives[p] > s, 0.4 * flats[p] + 0.3 * v1[p] + 0.2 * v2[p] + 0.1 * v3[p], flats[p])
                for p in range(LP)
            ]
        return flats

    def store(u, flats):
        @pl.when(u < units - per)
        def _():
            for p in range(LP):
                for r in range(2):
                    lam_a[r, u + per, p] = flats[p][:, r * cols:(r + 1) * cols]
            launch(u + per)

        @pl.when(u >= units - per)
        def _():
            group = u - (units - per)
            for p in range(LP):
                for r in range(2):
                    tmp[p, pl.ds(r, spec, stride=2), :] = flats[p][:, r * cols:(r + 1) * cols]
                outbuf[group, p] = tmp[p].astype(jnp.bfloat16)
            pltpu.make_async_copy(outbuf.at[group], out_hbm.at[group], out_sem.at[group]).start()

    def spread(k):
        to = lax.rem(lon + k, n_lon)
        return pltpu.make_async_remote_copy(
            src_ref=part.at[to], dst_ref=inbox1.at[lon], send_sem=s1.at[k], recv_sem=r1.at[lon],
            device_id=(lat, to), device_id_type=MESH)

    def spread_in(k):
        source = lax.rem(lon + k, n_lon)
        return source, pltpu.make_async_remote_copy(
            src_ref=part.at[source], dst_ref=inbox1.at[source], send_sem=s1.at[k], recv_sem=r1.at[source],
            device_id=(lat, source), device_id_type=MESH)

    def spread2(k):
        to = lax.rem(lat + k, n_lat)
        return pltpu.make_async_remote_copy(
            src_ref=turn.at[to], dst_ref=inbox2.at[lat], send_sem=s2.at[k], recv_sem=r2.at[lat],
            device_id=(to, lon), device_id_type=MESH)

    def spread2_in(k):
        source = lax.rem(lat + k, n_lat)
        return source, pltpu.make_async_remote_copy(
            src_ref=turn.at[source], dst_ref=inbox2.at[source], send_sem=s2.at[k], recv_sem=r2.at[source],
            device_id=(source, lon), device_id_type=MESH)

    def regions():
        lat8 = part.shape[1]
        contrib = jnp.concatenate([
            em_ref[pl.ds(r, spec, stride=2), :]
            * (lam_a[r, units - per, 0] + fin[:, r * cols:(r + 1) * cols])
            for r in range(2)], axis=1)
        where_from = jnp.concatenate([reg_ref[0:1, :], reg_ref[1:2, :]], axis=1)
        shape = (n_lon * lat8, 2 * cols)
        column = jnp.concatenate([jnp.full((lat8, 2 * cols), c, jnp.int32) for c in range(n_lon)], axis=0)
        band = lax.broadcasted_iota(jnp.int32, (lat8, 2 * cols), 0)
        band = jnp.concatenate([band] * n_lon, axis=0)
        onehot = (jnp.broadcast_to(where_from, shape) == band * n_lon + column).astype(jnp.float32)
        sums = lax.dot_general(
            onehot, contrib, (((1,), (1,)), ((), ())),
            precision=lax.Precision.HIGHEST, preferred_element_type=jnp.float32)
        for c in range(n_lon):
            part[c] = sums[c * lat8:(c + 1) * lat8]
        for k in range(1, n_lon):
            spread(k).start()

    def regions_turn():
        total = part[lon]
        for k in range(1, n_lon):
            source, copy = spread_in(k)
            copy.wait_recv()
            total = total + inbox1[source]
        for b in range(n_lat):
            turn[b] = total[b:b + 1]
        for k in range(1, n_lat):
            spread2(k).start()

    def regions_end():
        total = turn[lat]
        for k in range(1, n_lat):
            source, copy = spread2_in(k)
            copy.wait_recv()
            total = total + inbox2[source]
        grad_ref[...] = total

    @pl.when(jnp.logical_not(has_south))
    def _():
        south1[...] = jnp.zeros_like(south1)
        south2[...] = jnp.zeros_like(south2)

    loads[0].wait()
    for level in range(lev):
        p = level % LP
        tmp[p] = adj[level].astype(jnp.float32)
        for r in range(2):
            lam_a[r, level // LP, p] = tmp[p, pl.ds(r, spec, stride=2), :]

    pl.semaphore_wait(barrier, n_lon - 1 + n_lat - 1)
    launch(0)
    launch(1)
    inv_load.wait()
    for s in range(steps):
        for level in range(lev):
            mats[s, level] = inv[s, level].astype(jnp.float32).T.astype(jnp.bfloat16)
    first_step(0)
    for w in range(nwin):
        state_loads[w].wait()

    def body(u, carry):
        @pl.when(u + 2 < per)
        def _():
            launch(u + 2)

        @pl.when(u + 1 < units)
        def _():
            first_step(u + 1)
        flats = second_step(u)
        store(u, flats)

        @pl.when(u == units - per)
        def _():
            fin[...] = flats[0]
            regions()

        @pl.when(u == units - per + 2)
        def _():
            regions_turn()
        return carry

    lax.fori_loop(0, units, body, 0)
    regions_end()

    def drain(u, carry):
        @pl.when(has_north)
        def _():
            row_copy(0, u).wait_send()
            row_copy(1, u).wait_send()
        col_copy(0, u).wait_send()
        col_copy(1, u).wait_send()
        return carry

    lax.fori_loop(0, units, drain, 0)
    for k in range(1, n_lon):
        spread(k).wait_send()
    for k in range(1, n_lat):
        spread2(k).wait_send()
    for g in range(per):
        pltpu.make_async_copy(outbuf.at[g], out_hbm.at[g], out_sem.at[g]).wait()


def solution(mesh):
    n_lat, n_lon = mesh.shape["lat"], mesh.shape["lon"]

    def per_device(adjoint_in, state, inverses, courant_lon, courant_lat, emission, region_id, stiffness):
        lev, spec, rows, cols = adjoint_in.shape
        nwin, steps = state.shape[0], inverses.shape[0]
        per = lev // LP
        units = nwin * per
        lat8 = -(-n_lat // 8) * 8
        f32, bf16 = jnp.float32, jnp.bfloat16
        any_space = pl.BlockSpec(memory_space=pl.ANY)
        vmem = pl.BlockSpec(memory_space=pltpu.VMEM)
        halo = pltpu.VMEM((units, LP, spec, cols), f32)
        held = pltpu.VMEM((2, units, LP, spec, cols), f32)
        dma = pltpu.SemaphoreType.DMA
        out, grad = pl.pallas_call(
            functools.partial(kernel, n_lat, n_lon),
            out_shape=(
                jax.ShapeDtypeStruct((per, LP, rows * spec, cols), bf16),
                jax.ShapeDtypeStruct((1, spec), f32),
            ),
            in_specs=[any_space] * 3 + [vmem] * 5,
            out_specs=(any_space, vmem),
            scratch_shapes=[
                pltpu.VMEM((lev, rows * spec, cols), bf16),
                pltpu.VMEM((nwin, lev, rows * spec, cols), bf16),
                pltpu.VMEM(inverses.shape, bf16),
                pltpu.VMEM(inverses.shape, bf16),
                held, held, halo, halo, halo, halo, halo, halo,
                pltpu.VMEM((LP, rows * spec, cols), f32),
                pltpu.VMEM((spec, rows * cols), f32),
                pltpu.VMEM((per, LP, rows * spec, cols), bf16),
                pltpu.VMEM((3, rows, 8, cols), f32),
                pltpu.VMEM((n_lon, lat8, spec), f32),
                pltpu.VMEM((n_lon, lat8, spec), f32),
                pltpu.VMEM((n_lat, 1, spec), f32),
                pltpu.VMEM((n_lat, 1, spec), f32),
                dma, dma((nwin,)), dma, dma((per,)),
                dma((4, units)), dma((4, units)),
                dma((n_lon,)), dma((n_lon,)), dma((n_lat,)), dma((n_lat,)),
            ],
            compiler_params=pltpu.CompilerParams(collective_id=0, has_side_effects=True),
        )(
            adjoint_in.reshape(lev, spec * rows, cols),
            state.reshape(nwin, lev, spec * rows, cols),
            inverses, courant_lon, courant_lat,
            emission.reshape(spec * rows, cols), region_id, stiffness,
        )
        return out.reshape(adjoint_in.shape), grad

    in_specs = (
        P(None, None, "lat", "lon"),
        P(None, None, None, "lat", "lon"),
        P(),
        P("lat", "lon"),
        P("lat", "lon"),
        P(None, "lat", "lon"),
        P("lat", "lon"),
        P(None, "lat", "lon"),
    )
    out_specs = (P(None, None, "lat", "lon"), P(("lat", "lon"), None))
    return jax.shard_map(
        per_device, mesh=mesh, in_specs=in_specs, out_specs=out_specs, check_vma=False
    )
```

time: 119 us -> 54.7 us (0.46)
  Pallas kernels: 0 us -> 49.2 us
  blocking collectives: 41.4 us -> 0 us
  waiting for transfers between devices: 22.5 us -> 0 us
  local copies, waits for them, and re-layouts: 21.5 us -> 4.56 us
  starting transfers between devices: 13.6 us -> 0 us
  other arithmetic: 8.79 us -> 0 us
  matrix products: 7.96 us -> 0 us
  between operations: 2.85 us -> 0.65 us
    pallas_call x0 -> x1, Pallas kernels: none -> 49.2 us  [per_device(): pl.pallas_call(functools.partial(kernel, n_lat, n_lon), out_shape=(jax.Sh...]
    psum x1 -> x0, blocking collectives: 41.4 us -> none  [per_device(): total = lax.psum(partial_value, ('lat', 'lon'))]
    ppermute x8 -> x0, waiting for transfers between devices: 22.5 us -> none  [the longest x4 20.1 us: from_behind(): return lax.ppermute(block, axis, route)]
    ppermute x8 -> x0, starting transfers between devices: 13.6 us -> none  [the longest x4 8.34 us: shifted(): return lax.ppermute(block, axis, route)]
    slice x14 -> x0, local copies, waits for them, and re-layouts: 9.63 us -> none  [the longest x4 3.5 us: advect(): down = jnp.concatenate([lam[:, :, 1:, :], south], axis=2)]
    dot_general x19 -> x0, matrix products: 7.96 us -> none  [the longest x18 7.79 us: transposed(): lax.dot_general(mats, right_side, (((1,), (1,)), ((0,), (0,))), preferred...]
    ppermute x4 -> x0, local copies, waits for them, and re-layouts: 5.64 us -> none  [shifted(): return lax.ppermute(block, axis, route)]
    add x4 -> x0, other arithmetic: 5.51 us -> none  [the longest x3 5.49 us: advect(): return (1.0 - clon - clat) * lam + clat * down + clon * right]
  transfers between devices with their start and end apart: 8 -> 0, of which waited for: 6 -> 0; matrix products, arithmetic and copies ran while one was open for 12% -> 0% of each run, Pallas kernels for 0% -> 0%
where the time goes in v1:
time: 54.7 us; the launch traced here: 54.4 us
  Pallas kernels  49.2 us (90%)
  local copies, waits for them, and re-layouts  4.56 us (8%)
  between operations  0.65 us (1%)
    pallas_call x1, Pallas kernels, per_device(): pl.pallas_call(functools.partial(kernel, n_lat, n_lon), out_shape=(jax.Sh...  49.2 us
    unnamed x5, local copies, waits for them, and re-layouts  4.56 us

profile of v1, /device:TPU:0, one launch (start us, length us, event | category | flops | bytes accessed | tf_op | source)
XLA Modules:
  0.0 54.4 jit_solution(10735223306548694164)
XLA Ops:
  0.6 2.0 %copy.10.inv_hbm = bf16[3,8,100,100]{3,2,1,0:T(8,128)(2,1)} copy(bf16[3,8,100,100]{3,1,2,0:T(8,128)(2,1)} %param.10) | data formatting | bytes 960000 | tf_op args[2]
  2.6 49.2 %shard_map.95 = (bf16[4,2,200,128]{3,2,1,0:T(8,128)(2,1)}, f32[1,100]{1,0:T(1,128)}) custom-call(bf16[8,200,128]{2,1,0:T(8,128)(2,1)} %bitcast.5, bf16[2,8,200,128]{3,2,1,0:T(8,128)(2,1)} %bitcast.4, bf16[3,8,100,100]{3,2,1,0:T(8,128)(2,1)} %copy.10.inv_hbm, f32[2,128]{1,0:T(2,128)} %clon_ref.1, f32[2,128]{1,0:T(2,128)} %clat_ref.1, f32[200,128]{1,0:T(8,128)} %bitcast.7, ...), custom_call_target="tpu_custom_call" | custom-call | tf_op jit(solution)/shard_map/pallas_call | solution.py:309
  51.9 0.0 copy-start
  51.9 2.0 %copy.13 = bf16[8,100,2,128]{3,2,1,0:T(2,128)(2,1)} copy(bf16[8,100,2,128]{3,2,1,0:T(2,128)(2,1)} %bitcast.6) | data formatting | bytes 819200
  53.9 0.0 copy-done
  53.9 0.5 copy.14
Async XLA Ops:
  51.9 2.0 %copy-start = (f32[1,100]{1,0:T(1,128)S(1)}, f32[1,100]{1,0:T(1,128)}, u32[]{:S(2)}) copy-start(f32[1,100]{1,0:T(1,128)} %get-tuple-element.9) | copy-start | bytes 1204

commit v2 on v1

--- a/solution.py
+++ b/solution.py
@@ -9,15 +9,16 @@
 
 MESH = pl.DeviceIdType.MESH
 LP = 2
+AHEAD = 2
 
 
 def kernel(
     n_lat, n_lon,
-    adj_hbm, state_hbm, inv_hbm, clon_ref, clat_ref, em_ref, reg_ref, stiff_ref,
-    out_hbm, grad_ref,
-    adj, state, inv, mats, lam_a, lam_b, west1, west2, south1, south2, east1, east2,
-    tmp, fin, outbuf, coef, part, inbox1, turn, inbox2,
-    adj_sem, state_sem, inv_sem, out_sem, send_sem, recv_sem, s1, r1, s2, r2,
+    adj_hbm, state_hbm, inv_hbm, clon_hbm, clat_hbm, em_hbm, reg_hbm, stiff_hbm,
+    outbuf, grad_ref,
+    adj, state, inv, clon_ref, clat_ref, em_ref, reg_ref, stiff_ref, tall, mats, lam_a, lam_b, west1, west2, south1, south2, east1, east2,
+    tmp, fin, coef, part, inbox1, turn, inbox2,
+    adj_sem, state_sem, inv_sem, small_sem, send_sem, recv_sem, s1, r1, s2, r2,
 ):
     lev, rows2, cols = adj.shape
     nwin = state.shape[0]
@@ -31,27 +32,34 @@
     has_north = lat > 0
     has_south = lat < n_lat - 1
 
-    loads = [pltpu.make_async_copy(adj_hbm, adj, adj_sem)]
-    loads[0].start()
+    barrier = pltpu.get_barrier_semaphore()
+    for k in range(1, n_lon):
+        pl.semaphore_signal(barrier, inc=1, device_id=(lat, lax.rem(lon + k, n_lon)), device_id_type=MESH)
+    for k in range(1, n_lat):
+        pl.semaphore_signal(barrier, inc=1, device_id=(lax.rem(lat + k, n_lat), lon), device_id_type=MESH)
+
+    adj_loads = [
+        pltpu.make_async_copy(
+            adj_hbm.at[pl.ds(u * LP, LP)], adj.at[pl.ds(u * LP, LP)], adj_sem.at[u])
+        for u in range(per)
+    ]
+    for load in adj_loads:
+        load.start()
     inv_load = pltpu.make_async_copy(inv_hbm, inv, inv_sem)
     inv_load.start()
+    small = [
+        pltpu.make_async_copy(src, dst, small_sem.at[n])
+        for n, (src, dst) in enumerate((
+            (clon_hbm, clon_ref), (clat_hbm, clat_ref), (stiff_hbm, stiff_ref),
+            (reg_hbm, reg_ref), (em_hbm, em_ref)))
+    ]
+    for load in small:
+        load.start()
     state_loads = [
         pltpu.make_async_copy(state_hbm.at[w], state.at[w], state_sem.at[w]) for w in range(nwin)
     ]
     for w in reversed(range(nwin)):
         state_loads[w].start()
-
-    barrier = pltpu.get_barrier_semaphore()
-    for k in range(1, n_lon):
-        pl.semaphore_signal(barrier, inc=1, device_id=(lat, lax.rem(lon + k, n_lon)), device_id_type=MESH)
-    for k in range(1, n_lat):
-        pl.semaphore_signal(barrier, inc=1, device_id=(lax.rem(lat + k, n_lat), lon), device_id_type=MESH)
-
-    for r in range(2):
-        clon, clat = clon_ref[r:r + 1, :], clat_ref[r:r + 1, :]
-        coef[0, r] = jnp.broadcast_to(1.0 - clon - clat, (8, cols))
-        coef[1, r] = jnp.broadcast_to(clat, (8, cols))
-        coef[2, r] = jnp.broadcast_to(clon, (8, cols))
 
     lane = lax.broadcasted_iota(jnp.int32, (spec, cols), 1)
 
@@ -161,7 +169,6 @@
                 for r in range(2):
                     tmp[p, pl.ds(r, spec, stride=2), :] = flats[p][:, r * cols:(r + 1) * cols]
                 outbuf[group, p] = tmp[p].astype(jnp.bfloat16)
-            pltpu.make_async_copy(outbuf.at[group], out_hbm.at[group], out_sem.at[group]).start()
 
     def spread(k):
         to = lax.rem(lon + k, n_lon)
@@ -226,37 +233,54 @@
             total = total + inbox2[source]
         grad_ref[...] = total
 
+    def take(u):
+        adj_loads[u].wait()
+        for p in range(LP):
+            tmp[p] = adj[u * LP + p].astype(jnp.float32)
+            for r in range(2):
+                lam_a[r, u, p] = tmp[p, pl.ds(r, spec, stride=2), :]
+
+    take(0)
+    pl.semaphore_wait(barrier, n_lon - 1 + n_lat - 1)
+    launch(0)
+    for u in range(1, AHEAD + 1):
+        take(u)
+        launch(u)
+
     @pl.when(jnp.logical_not(has_south))
     def _():
         south1[...] = jnp.zeros_like(south1)
         south2[...] = jnp.zeros_like(south2)
 
-    loads[0].wait()
-    for level in range(lev):
-        p = level % LP
-        tmp[p] = adj[level].astype(jnp.float32)
-        for r in range(2):
-            lam_a[r, level // LP, p] = tmp[p, pl.ds(r, spec, stride=2), :]
-
-    pl.semaphore_wait(barrier, n_lon - 1 + n_lat - 1)
-    launch(0)
-    launch(1)
+    for load in small:
+        load.wait()
+    for r in range(2):
+        clon, clat = clon_ref[r:r + 1, :], clat_ref[r:r + 1, :]
+        coef[0, r] = jnp.broadcast_to(1.0 - clon - clat, (8, cols))
+        coef[1, r] = jnp.broadcast_to(clat, (8, cols))
+        coef[2, r] = jnp.broadcast_to(clon, (8, cols))
+
+    first_step(0)
+    for u in range(AHEAD + 1, per):
+        take(u)
     inv_load.wait()
     for s in range(steps):
+        tall[...] = inv[s].astype(jnp.float32)
         for level in range(lev):
-            mats[s, level] = inv[s, level].astype(jnp.float32).T.astype(jnp.bfloat16)
-    first_step(0)
+            mats[s, level] = tall[pl.ds(level, spec, stride=lev), :].T.astype(jnp.bfloat16)
+    for u in range(1, AHEAD):
+        first_step(u)
     for w in range(nwin):
         state_loads[w].wait()
 
     def body(u, carry):
-        @pl.when(u + 2 < per)
-        def _():
-            launch(u + 2)
-
-        @pl.when(u + 1 < units)
-        def _():
-            first_step(u + 1)
+        @pl.when(u + AHEAD + 1 < per)
+        def _():
+            launch(u + AHEAD + 1)
+
+        @pl.when(u + AHEAD < units)
+        def _():
+            first_step(u + AHEAD)
         flats = second_step(u)
         store(u, flats)
 
@@ -265,7 +289,7 @@
             fin[...] = flats[0]
             regions()
 
-        @pl.when(u == units - per + 2)
+        @pl.when(u == units - per + 4 // LP)
         def _():
             regions_turn()
         return carry
@@ -287,8 +311,17 @@
         spread(k).wait_send()
     for k in range(1, n_lat):
         spread2(k).wait_send()
-    for g in range(per):
-        pltpu.make_async_copy(outbuf.at[g], out_hbm.at[g], out_sem.at[g]).wait()
+
+
+def finish(held_ref, grad_ref, out_hbm, grad_hbm, sems):
+    copies = [
+        pltpu.make_async_copy(held_ref, out_hbm, sems.at[0]),
+        pltpu.make_async_copy(grad_ref, grad_hbm, sems.at[1]),
+    ]
+    for copy in copies:
+        copy.start()
+    for copy in copies:
+        copy.wait()
 
 
 def solution(mesh):
@@ -309,26 +342,31 @@
         out, grad = pl.pallas_call(
             functools.partial(kernel, n_lat, n_lon),
             out_shape=(
-                jax.ShapeDtypeStruct((per, LP, rows * spec, cols), bf16),
-                jax.ShapeDtypeStruct((1, spec), f32),
+                pltpu.VMEM((per, LP, rows * spec, cols), bf16),
+                pltpu.VMEM((1, spec), f32),
             ),
-            in_specs=[any_space] * 3 + [vmem] * 5,
-            out_specs=(any_space, vmem),
+            in_specs=[any_space] * 8,
+            out_specs=(vmem, vmem),
             scratch_shapes=[
                 pltpu.VMEM((lev, rows * spec, cols), bf16),
                 pltpu.VMEM((nwin, lev, rows * spec, cols), bf16),
-                pltpu.VMEM(inverses.shape, bf16),
+                pltpu.VMEM((steps, spec * lev, spec), bf16),
+                pltpu.VMEM(courant_lon.shape, f32),
+                pltpu.VMEM(courant_lat.shape, f32),
+                pltpu.VMEM((spec * rows, cols), f32),
+                pltpu.VMEM(region_id.shape, jnp.int32),
+                pltpu.VMEM(stiffness.shape, jnp.int32),
+                pltpu.VMEM((spec * lev, spec), f32),
                 pltpu.VMEM(inverses.shape, bf16),
                 held, held, halo, halo, halo, halo, halo, halo,
                 pltpu.VMEM((LP, rows * spec, cols), f32),
                 pltpu.VMEM((spec, rows * cols), f32),
-                pltpu.VMEM((per, LP, rows * spec, cols), bf16),
                 pltpu.VMEM((3, rows, 8, cols), f32),
                 pltpu.VMEM((n_lon, lat8, spec), f32),
                 pltpu.VMEM((n_lon, lat8, spec), f32),
                 pltpu.VMEM((n_lat, 1, spec), f32),
                 pltpu.VMEM((n_lat, 1, spec), f32),
-                dma, dma((nwin,)), dma, dma((per,)),
+                dma((per,)), dma((nwin,)), dma, dma((5,)),
                 dma((4, units)), dma((4, units)),
                 dma((n_lon,)), dma((n_lon,)), dma((n_lat,)), dma((n_lat,)),
             ],
@@ -336,9 +374,19 @@
         )(
             adjoint_in.reshape(lev, spec * rows, cols),
             state.reshape(nwin, lev, spec * rows, cols),
-            inverses, courant_lon, courant_lat,
+            inverses.transpose(0, 2, 1, 3).reshape(steps, spec * lev, spec), courant_lon, courant_lat,
             emission.reshape(spec * rows, cols), region_id, stiffness,
         )
+        out, grad = pl.pallas_call(
+            finish,
+            out_shape=(
+                jax.ShapeDtypeStruct(out.shape, bf16),
+                jax.ShapeDtypeStruct(grad.shape, f32),
+            ),
+            in_specs=[any_space] * 2,
+            out_specs=(any_space, any_space),
+            scratch_shapes=[dma((2,))],
+        )(*(pltpu.with_memory_space_constraint(x, pltpu.VMEM) for x in (out, grad)))
         return out.reshape(adjoint_in.shape), grad
 
     in_specs = (

time: 54.7 us -> 48.3 us (0.88)
  local copies, waits for them, and re-layouts: 4.56 us -> 0 us
  Pallas kernels: 49.2 us -> 47.5 us
    unnamed x5 -> x0, local copies, waits for them, and re-layouts: 4.56 us -> none
    pallas_call x1 -> x2, Pallas kernels: 49.2 us -> 47.5 us  [the longest x1 46.7 us: per_device(): pl.pallas_call(functools.partial(kernel, n_lat, n_lon), out_shape=(pltpu....]
where the time goes in v2:
time: 48.3 us; the launch traced here: 48.2 us
  Pallas kernels  47.5 us (98%)
  between operations  0.64 us (1%)
    pallas_call x1, Pallas kernels, per_device(): pl.pallas_call(functools.partial(kernel, n_lat, n_lon), out_shape=(pltpu....  46.7 us

profile of v2, /device:TPU:0, one launch (start us, length us, event | category | flops | bytes accessed | tf_op | source)
XLA Modules:
  0.0 48.2 jit_solution(18095697151677690912)
XLA Ops:
  0.6 46.7 %shard_map.95 = (bf16[4,2,200,128]{3,2,1,0:T(8,128)(2,1)S(1)}, f32[1,100]{1,0:T(1,128)S(1)}) custom-call(bf16[8,200,128]{2,1,0:T(8,128)(2,1)} %bitcast.9, bf16[2,8,200,128]{3,2,1,0:T(8,128)(2,1)} %bitcast.7, bf16[3,800,100]{2,1,0:T(8,128)(2,1)} %bitcast.8, f32[2,128]{1,0:T(2,128)} %clon_hbm.1, f32[2,128]{1,0:T(2,128)} %clat_hbm.1, f32[200,128]{1,0:T(8,128)} %bitcast.10, ...), custom_call_target="tpu_custom_call" | custom-call | tf_op jit(solution)/shard_map/pallas_call | solution.py:342
  47.4 0.8 %shard_map.96 = (bf16[4,2,200,128]{3,2,1,0:T(8,128)(2,1)}, f32[1,100]{1,0:T(1,128)}) custom-call(bf16[4,2,200,128]{3,2,1,0:T(8,128)(2,1)S(1)} %get-tuple-element.6.held_ref, f32[1,100]{1,0:T(1,128)S(1)} %get-tuple-element.7.grad_ref), custom_call_target="tpu_custom_call" | custom-call | tf_op jit(solution)/shard_map/pallas_call | solution.py:380

commit v3 on v2

--- a/solution.py
+++ b/solution.py
@@ -289,7 +289,7 @@
             fin[...] = flats[0]
             regions()
 
-        @pl.when(u == units - per + 4 // LP)
+        @pl.when(u == units - per + 1)
         def _():
             regions_turn()
         return carry

time: 48.3 us -> 46.9 us (0.971)
  Pallas kernels: 47.5 us -> 46.1 us
    pallas_call x1, Pallas kernels: 46.7 us -> 45.3 us  [per_device(): pl.pallas_call(functools.partial(kernel, n_lat, n_lon), out_shape=(pltpu....]
where the time goes in v3:
time: 46.9 us; the launch traced here: 46.7 us
  Pallas kernels  46.1 us (98%)
  between operations  0.64 us (1%)
    pallas_call x1, Pallas kernels, per_device(): pl.pallas_call(functools.partial(kernel, n_lat, n_lon), out_shape=(pltpu....  45.3 us

profile of v3, /device:TPU:0, one launch (start us, length us, event | category | flops | bytes accessed | tf_op | source)
XLA Modules:
  0.0 46.7 jit_solution(16303830869791319119)
XLA Ops:
  0.6 45.3 %shard_map.95 = (bf16[4,2,200,128]{3,2,1,0:T(8,128)(2,1)S(1)}, f32[1,100]{1,0:T(1,128)S(1)}) custom-call(bf16[8,200,128]{2,1,0:T(8,128)(2,1)} %bitcast.9, bf16[2,8,200,128]{3,2,1,0:T(8,128)(2,1)} %bitcast.7, bf16[3,800,100]{2,1,0:T(8,128)(2,1)} %bitcast.8, f32[2,128]{1,0:T(2,128)} %clon_hbm.1, f32[2,128]{1,0:T(2,128)} %clat_hbm.1, f32[200,128]{1,0:T(8,128)} %bitcast.10, ...), custom_call_target="tpu_custom_call" | custom-call | tf_op jit(solution)/shard_map/pallas_call | solution.py:342
  46.0 0.8 %shard_map.96 = (bf16[4,2,200,128]{3,2,1,0:T(8,128)(2,1)}, f32[1,100]{1,0:T(1,128)}) custom-call(bf16[4,2,200,128]{3,2,1,0:T(8,128)(2,1)S(1)} %get-tuple-element.6.held_ref, f32[1,100]{1,0:T(1,128)S(1)} %get-tuple-element.7.grad_ref), custom_call_target="tpu_custom_call" | custom-call | tf_op jit(solution)/shard_map/pallas_call | solution.py:380
